TPU v7x, 32 devices: a whole 2x2x4 slice. The times are simulated.
32 devices in a mesh: tm: 4 (over y, x), space: 8 (over z, core).
Axes of the slice: x: 2, y: 2, z: 4, core: 2. Of those that a mesh axis runs over, the one named last changes fastest.
Arguments:
- initial_state: float32 [3, 192, 256], P(None, 'space'), may hold values from -2 to 2
- c_guess: float32 [4, 3, 192, 256], P('tm', None, 'space'), may hold values from -2 to 2
- friction: float32 [192, 256], P('space'), may hold values from 0.05 to 1
Outputs:
- c_points: float32 [4, 3, 192, 256], P('tm', None, 'space')
- f_points: float32 [4, 3, 192, 256], P('tm', None, 'space')
All inputs are finite; a program needn't handle non-finite values.
Results may differ from a plain program's by a relative error of at most 0.00012.
Values sent between devices are 32-bit elements; how exact they have to be, the bound alone decides.
No kernel may reach another device: no remote copies, remote signals or barrier semaphores. Data moves between devices by JAX's collectives and lax.ppermute only.
A program may use at most 64 MiB of HBM per device.

v0:
```python
import jax
import jax.numpy as jnp
from jax import lax
from jax.sharding import PartitionSpec as P

STEPS = 8
gravity = 2.0
coriolis = 0.5
viscosity = 0.5
time_step = 0.04


def with_halo(block, sides, width):
    for axis, dim in sides:
        count = lax.axis_size(axis)
        forward = [(i, i + 1) for i in range(count - 1)]
        forward.append((count - 1, 0))
        backward = [(target, source) for source, target in forward]
        low = lax.ppermute(
            lax.slice_in_dim(block, block.shape[dim] - width, None, axis=dim), axis, forward
        )
        high = lax.ppermute(lax.slice_in_dim(block, 0, width, axis=dim), axis, backward)
        block = jnp.concatenate([low, block, high], axis=dim)
    return block


def shifted(value, axis, by):
    size = lax.axis_size(axis)
    pairs = [(i, i + by) for i in range(size) if 0 <= i + by < size]
    return lax.ppermute(value, axis, pairs)


def cut_neighbours(field):
    return (
        field[2:],
        field[:-2],
        jnp.roll(field, -1, 1)[1:-1],
        jnp.roll(field, 1, 1)[1:-1],
        field[1:-1],
    )


def spread(near):
    return near[0] + near[1] + near[2] + near[3] - 4.0 * near[4]


def tendency(fields, drag, neighbours):
    height = fields[0]
    row_vel = fields[1]
    col_vel = fields[2]
    height_near = neighbours(height)
    row_near = neighbours(row_vel)
    col_near = neighbours(col_vel)
    flux_row = neighbours((1.0 + height) * row_vel)
    flux_col = neighbours((1.0 + height) * col_vel)
    row_mid = row_near[4]
    col_mid = col_near[4]
    rate_height = -(
        0.5 * (flux_row[0] - flux_row[1]) + 0.5 * (flux_col[2] - flux_col[3])
    ) + viscosity * spread(height_near)
    rate_row = (
        -(
            row_mid * (0.5 * (row_near[0] - row_near[1]))
            + col_mid * (0.5 * (row_near[2] - row_near[3]))
        )
        - gravity * (0.5 * (height_near[0] - height_near[1]))
        + coriolis * col_mid
        - drag * row_mid
        + viscosity * spread(row_near)
    )
    rate_col = (
        -(
            row_mid * (0.5 * (col_near[0] - col_near[1]))
            + col_mid * (0.5 * (col_near[2] - col_near[3]))
        )
        - gravity * (0.5 * (height_near[2] - height_near[3]))
        - coriolis * row_mid
        - drag * col_mid
        + viscosity * spread(col_near)
    )
    return jnp.stack([rate_height, rate_row, rate_col])


def trim_rows(array, width):
    return array[..., width : array.shape[-2] - width, :]


def heun_step(fields, drag, size):
    slope_one = tendency(fields, drag[1:-1], cut_neighbours)
    midpoint = fields[:, 1:-1] + size * slope_one
    slope_two = tendency(midpoint, drag[2:-2], cut_neighbours)
    return fields[:, 2:-2] + 0.5 * size * (slope_one[:, 1:-1] + slope_two)


def advance(fields, drag_pad, step_count, layers, with_coarse):
    coarse = fields
    reaches = [layers] * (step_count // layers)
    if step_count % layers:
        reaches = reaches + [step_count % layers]
    for group, reach in enumerate(reaches):
        padded = with_halo(fields, (("space", 1),), 2 * reach)
        drag = trim_rows(drag_pad, 8 - 2 * reach)
        if with_coarse and group == 0:
            coarse = trim_rows(heun_step(padded, drag, STEPS * time_step), 2 * reach - 2)
        for repeat in range(reach):
            padded = heun_step(padded, drag, time_step)
            drag = trim_rows(drag, 2)
        fields = padded
    return (fields, coarse)


def body(initial_state, c_guess, friction):
    slice_index = lax.axis_index("tm")
    coarse_step = STEPS * time_step
    layers = 4
    drag_pad = with_halo(friction, (("space", 0),), 8)

    def earlier(fields):
        incoming = shifted(fields, "tm", 1)
        return jnp.where(slice_index == 0, initial_state, incoming)

    relaxed, unused = advance(earlier(c_guess[0]), drag_pad, STEPS, layers, False)
    fine_end, coarse_end = advance(earlier(relaxed), drag_pad, STEPS, layers, True)
    defect = fine_end - coarse_end
    defect_pad = with_halo(defect, (("space", 1),), 8)
    gathered = lax.all_gather(defect_pad[None], "tm", axis=0, tiled=True)

    def group_fn(group, carry):
        current, owned = carry
        padded = with_halo(current, (("space", 1),), 8)
        drag = drag_pad
        for offset in range(4):
            turn = group * 4 + offset
            defect_now = trim_rows(
                lax.dynamic_index_in_dim(gathered, turn, 0, keepdims=False), 2 * offset + 2
            )
            padded = heun_step(padded, drag, coarse_step) + defect_now
            drag = trim_rows(drag, 2)
            owned = jnp.where(turn == slice_index, trim_rows(padded, 6 - 2 * offset), owned)
        return (padded, owned)

    unused_state, c_points = lax.fori_loop(
        0, lax.axis_size("tm") // 4, group_fn, (initial_state, jnp.zeros_like(defect))
    )
    f_points, unused_end = advance(earlier(c_points), drag_pad, STEPS - 1, layers, False)
    return (c_points[None], f_points[None])


def solution(mesh):
    placed = (P(None, "space", None), P("tm", None, "space", None), P("space", None))
    return jax.shard_map(
        body,
        mesh=mesh,
        in_specs=placed,
        out_specs=(P("tm", None, "space", None), P("tm", None, "space", None)),
        check_vma=False,
    )
```

profile of v0, /device:TPU:4, one launch (start us, length us, event | category | flops | bytes accessed | tf_op | source)
XLA Modules:
  0.0 128.7 jit_solution(17374172756652679504)
XLA Ops:
  0.6 0.8 fusion.2103
  1.4 0.8 fusion.1657
  2.2 1.7 %collective-permute-start = (f32[3,8,256]{2,1,0:T(8,128)S(1)}, f32[3,8,256]{2,1,0:T(8,128)S(1)}, u32[]{:S(2)}, u32[]{:S(2)}) collective-permute-start(f32[3,8,256]{2,1,0:T(8,128)S(1)} %get-tuple-element.361), channel_id=1, source_target_pairs={{0,1},{1,2},{2,3},{3,4},{4,5},{5,6},{6,7},{7,0},{8,9},{9,10},{10,1... | collective-permute-start | bytes 73736 | tf_op jit(solution)/shard_map/while/body/eval_jaxpr/ppermute | solution.py:19
  3.8 3.4 %collective-permute-start.4 = (f32[3,24,256]{2,1,0:T(8,128)S(1)}, f32[3,24,256]{2,1,0:T(8,128)S(1)}, u32[]{:S(2)}, u32[]{:S(2)}) collective-permute-start(f32[3,24,256]{2,1,0:T(8,128)S(1)} %bitcast.5615), channel_id=1, source_target_pairs={{0,8},{8,16},{16,24},{1,9},{9,17},{17,25},{2,10},{10,18},{18,26},{... | collective-permute-start | bytes 221192 | tf_op jit(solution)/shard_map/ppermute | solution.py:30
  7.2 1.6 %collective-permute-start.3 = (f32[8,256]{1,0:T(8,128)S(1)}, f32[8,256]{1,0:T(8,128)S(1)}, u32[]{:S(2)}, u32[]{:S(2)}) collective-permute-start(f32[8,256]{1,0:T(8,128)S(1)} %get-tuple-element.1254), channel_id=1, source_target_pairs={{1,0},{2,1},{3,2},{4,3},{5,4},{6,5},{7,6},{0,7},{9,8},{10,9},{11,1... | collective-permute-start | bytes 24584 | tf_op jit(solution)/shard_map/ppermute | solution.py:22
  8.9 0.8 collective-permute-start.1
  9.7 0.6 collective-permute-done.3
  10.3 0.7 collective-permute-done.4
  11.0 0.2 collective-permute-done.1
  12.3 3.6 %collective-permute-start.6 = (f32[3,8,256]{2,1,0:T(8,128)S(1)}, f32[3,8,256]{2,1,0:T(8,128)S(1)}, u32[]{:S(2)}, u32[]{:S(2)}) collective-permute-start(f32[3,8,256]{2,1,0:T(8,128)S(1)} %get-tuple-element.373), channel_id=1, source_target_pairs={{1,0},{2,1},{3,2},{4,3},{5,4},{6,5},{7,6},{0,7},{9,8},{10,9},{11,1... | collective-permute-start | bytes 73736 | tf_op jit(solution)/shard_map/ppermute | solution.py:22
  16.3 1.1 collective-permute-done.6
  17.4 3.5 %collective-permute-done.5 = f32[3,8,256]{2,1,0:T(8,128)S(1)} collective-permute-done((f32[3,8,256]{2,1,0:T(8,128)S(1)}, f32[3,8,256]{2,1,0:T(8,128)S(1)}, u32[]{:S(2)}, u32[]{:S(2)}) %collective-permute-start.5) | collective-permute-done | bytes 24608 | tf_op jit(solution)/shard_map/ppermute | solution.py:19
  22.6 0.1 fusion.564
  23.6 0.1 fusion.544
  28.9 0.5 collective-permute-start.7
  29.4 0.9 collective-permute-done.8
  30.4 3.6 %collective-permute-done.7 = f32[3,8,256]{2,1,0:T(8,128)S(1)} collective-permute-done((f32[3,8,256]{2,1,0:T(8,128)S(1)}, f32[3,8,256]{2,1,0:T(8,128)S(1)}, u32[]{:S(2)}, u32[]{:S(2)}) %collective-permute-start.7) | collective-permute-done | bytes 24608 | tf_op jit(solution)/shard_map/ppermute | solution.py:19
  34.8 0.1 fusion.524
  35.8 0.1 fusion.504
  36.8 0.1 fusion.484
  42.0 1.9 %collective-permute-start.9 = (f32[3,24,256]{2,1,0:T(8,128)S(1)}, f32[3,24,256]{2,1,0:T(8,128)S(1)}, u32[]{:S(2)}, u32[]{:S(2)}) collective-permute-start(f32[3,24,256]{2,1,0:T(8,128)S(1)} %fusion.57), channel_id=1, source_target_pairs={{0,8},{8,16},{16,24},{1,9},{9,17},{17,25},{2,10},{10,18},{18,26},{... | collective-permute-start | bytes 221192 | tf_op jit(solution)/shard_map/ppermute | solution.py:30
  44.0 0.1 fusion.604
  44.1 5.1 %collective-permute-done.9 = f32[3,24,256]{2,1,0:T(8,128)S(1)} collective-permute-done((f32[3,24,256]{2,1,0:T(8,128)S(1)}, f32[3,24,256]{2,1,0:T(8,128)S(1)}, u32[]{:S(2)}, u32[]{:S(2)}) %collective-permute-start.9) | collective-permute-done | bytes 73760 | tf_op jit(solution)/shard_map/ppermute | solution.py:30
  49.3 0.5 collective-permute-start.10
  49.8 0.9 collective-permute-done.11
  50.8 3.6 %collective-permute-done.10 = f32[3,8,256]{2,1,0:T(8,128)S(1)} collective-permute-done((f32[3,8,256]{2,1,0:T(8,128)S(1)}, f32[3,8,256]{2,1,0:T(8,128)S(1)}, u32[]{:S(2)}, u32[]{:S(2)}) %collective-permute-start.10) | collective-permute-done | bytes 24608 | tf_op jit(solution)/shard_map/ppermute | solution.py:19
  56.8 0.1 fusion.444
  63.2 0.5 collective-permute-start.12
  63.8 0.1 fusion.344
  64.0 0.7 collective-permute-done.13
  64.7 3.7 %collective-permute-done.12 = f32[3,8,256]{2,1,0:T(8,128)S(1)} collective-permute-done((f32[3,8,256]{2,1,0:T(8,128)S(1)}, f32[3,8,256]{2,1,0:T(8,128)S(1)}, u32[]{:S(2)}, u32[]{:S(2)}) %collective-permute-start.12) | collective-permute-done | bytes 24608 | tf_op jit(solution)/shard_map/ppermute | solution.py:19
  69.3 0.1 fusion.136
  70.3 0.1 fusion.384
  71.3 0.1 fusion.364
  76.6 0.5 collective-permute-start.14
  77.2 0.9 collective-permute-done.15
  78.1 3.6 %collective-permute-done.14 = f32[3,8,256]{2,1,0:T(8,128)S(1)} collective-permute-done((f32[3,8,256]{2,1,0:T(8,128)S(1)}, f32[3,8,256]{2,1,0:T(8,128)S(1)}, u32[]{:S(2)}, u32[]{:S(2)}) %collective-permute-start.14) | collective-permute-done | bytes 24608 | tf_op jit(solution)/shard_map/ppermute | solution.py:19
  81.7 8.7 %all-gather = f32[12,40,256]{2,1,0:T(8,128)S(1)} all-gather(f32[3,40,256]{2,1,0:T(8,128)S(1)} %pad_maximum_fusion.13), channel_id=2, replica_groups=mesh['tm'=4,'space'=8] {'tm'}, dimensions={0}, use_global_device_ids=true | all-gather | bytes 614400 | tf_op jit(solution)/shard_map/all_gather | solution.py:126
  96.5 3.6 %collective-permute-start.16 = (f32[3,24,256]{2,1,0:T(8,128)S(1)}, f32[3,24,256]{2,1,0:T(8,128)S(1)}, u32[]{:S(2)}, u32[]{:S(2)}) collective-permute-start(f32[3,24,256]{2,1,0:T(8,128)S(1)} %fusion.47), channel_id=1, source_target_pairs={{0,8},{8,16},{16,24},{1,9},{9,17},{17,25},{2,10},{10,18},{18,26},{... | collective-permute-start | bytes 221192 | tf_op jit(solution)/shard_map/ppermute | solution.py:30
  100.1 3.5 %collective-permute-done.16 = f32[3,24,256]{2,1,0:T(8,128)S(1)} collective-permute-done((f32[3,24,256]{2,1,0:T(8,128)S(1)}, f32[3,24,256]{2,1,0:T(8,128)S(1)}, u32[]{:S(2)}, u32[]{:S(2)}) %collective-permute-start.16) | collective-permute-done | bytes 73760 | tf_op jit(solution)/shard_map/ppermute | solution.py:30
  103.7 0.5 collective-permute-start.17
  104.2 1.0 collective-permute-done.18
  105.3 3.6 %collective-permute-done.17 = f32[3,8,256]{2,1,0:T(8,128)S(1)} collective-permute-done((f32[3,8,256]{2,1,0:T(8,128)S(1)}, f32[3,8,256]{2,1,0:T(8,128)S(1)}, u32[]{:S(2)}, u32[]{:S(2)}) %collective-permute-start.17) | collective-permute-done | bytes 24608 | tf_op jit(solution)/shard_map/ppermute | solution.py:19
  110.6 0.1 fusion.284
  117.0 0.5 collective-permute-start.19
  117.5 1.0 collective-permute-done.20
  118.5 3.6 %collective-permute-done.19 = f32[3,6,256]{2,1,0:T(8,128)S(1)} collective-permute-done((f32[3,6,256]{2,1,0:T(8,128)S(1)}, f32[3,6,256]{2,1,0:T(8,128)S(1)}, u32[]{:S(2)}, u32[]{:S(2)}) %collective-permute-start.19) | collective-permute-done | bytes 18464 | tf_op jit(solution)/shard_map/ppermute | solution.py:19
  128.0 0.7 fusion.42
  (792 shorter events, 52.2 us)
Async XLA Ops:
  0.6 3.2 %copy-start.3 = (f32[1,3,24,256]{3,2,1,0:T(8,128)S(1)}, f32[1,3,24,256]{3,2,1,0:T(8,128)}, u32[]{:S(2)}) copy-start(f32[1,3,24,256]{3,2,1,0:T(8,128)} %param.4) | copy-start | bytes 221188
  1.4 8.3 %collective-permute-start.2 = (f32[8,256]{1,0:T(8,128)S(1)}, f32[8,256]{1,0:T(8,128)S(1)}, u32[]{:S(2)}, u32[]{:S(2)}) collective-permute-start(f32[8,256]{1,0:T(8,128)S(1)} %get-tuple-element.1255), channel_id=1, source_target_pairs={{0,1},{1,2},{2,3},{3,4},{4,5},{5,6},{6,7},{7,0},{8,9},{9,10},{10,1... | collective-permute-start | bytes 24584 | tf_op jit(solution)/shard_map/ppermute | solution.py:19
  2.2 7.5 %copy-start = (f32[24,256]{1,0:T(8,128)S(1)}, f32[24,256]{1,0:T(8,128)}, u32[]{:S(2)}) copy-start(f32[24,256]{1,0:T(8,128)} %param.5) | copy-start | bytes 73732
  2.2 8.1 %collective-permute-start = (f32[3,8,256]{2,1,0:T(8,128)S(1)}, f32[3,8,256]{2,1,0:T(8,128)S(1)}, u32[]{:S(2)}, u32[]{:S(2)}) collective-permute-start(f32[3,8,256]{2,1,0:T(8,128)S(1)} %get-tuple-element.361), channel_id=1, source_target_pairs={{0,1},{1,2},{2,3},{3,4},{4,5},{5,6},{6,7},{7,0},{8,9},{9,10},{10,1... | collective-permute-start | bytes 73736 | tf_op jit(solution)/shard_map/while/body/eval_jaxpr/ppermute | solution.py:19
  3.8 7.1 %collective-permute-start.4 = (f32[3,24,256]{2,1,0:T(8,128)S(1)}, f32[3,24,256]{2,1,0:T(8,128)S(1)}, u32[]{:S(2)}, u32[]{:S(2)}) collective-permute-start(f32[3,24,256]{2,1,0:T(8,128)S(1)} %bitcast.5615), channel_id=1, source_target_pairs={{0,8},{8,16},{16,24},{1,9},{9,17},{17,25},{2,10},{10,18},{18,26},{... | collective-permute-start | bytes 221192 | tf_op jit(solution)/shard_map/ppermute | solution.py:30
  7.2 3.0 %collective-permute-start.3 = (f32[8,256]{1,0:T(8,128)S(1)}, f32[8,256]{1,0:T(8,128)S(1)}, u32[]{:S(2)}, u32[]{:S(2)}) collective-permute-start(f32[8,256]{1,0:T(8,128)S(1)} %get-tuple-element.1254), channel_id=1, source_target_pairs={{1,0},{2,1},{3,2},{4,3},{5,4},{6,5},{7,6},{0,7},{9,8},{10,9},{11,1... | collective-permute-start | bytes 24584 | tf_op jit(solution)/shard_map/ppermute | solution.py:22
  8.9 2.3 %collective-permute-start.1 = (f32[3,8,256]{2,1,0:T(8,128)S(1)}, f32[3,8,256]{2,1,0:T(8,128)S(1)}, u32[]{:S(2)}, u32[]{:S(2)}) collective-permute-start(f32[3,8,256]{2,1,0:T(8,128)S(1)} %get-tuple-element.360), channel_id=1, source_target_pairs={{1,0},{2,1},{3,2},{4,3},{5,4},{6,5},{7,6},{0,7},{9,8},{10,9},{11,1... | collective-permute-start | bytes 73736 | tf_op jit(solution)/shard_map/while/body/eval_jaxpr/ppermute | solution.py:22
  9.7 1.3 %copy-start.1 = (f32[3,24,256]{2,1,0:T(8,128)S(1)}, f32[3,24,256]{2,1,0:T(8,128)}, u32[]{:S(2)}) copy-start(f32[3,24,256]{2,1,0:T(8,128)} %param.3) | copy-start | bytes 221188
  12.3 5.1 %collective-permute-start.6 = (f32[3,8,256]{2,1,0:T(8,128)S(1)}, f32[3,8,256]{2,1,0:T(8,128)S(1)}, u32[]{:S(2)}, u32[]{:S(2)}) collective-permute-start(f32[3,8,256]{2,1,0:T(8,128)S(1)} %get-tuple-element.373), channel_id=1, source_target_pairs={{1,0},{2,1},{3,2},{4,3},{5,4},{6,5},{7,6},{0,7},{9,8},{10,9},{11,1... | collective-permute-start | bytes 73736 | tf_op jit(solution)/shard_map/ppermute | solution.py:22
  15.8 5.0 %collective-permute-start.5 = (f32[3,8,256]{2,1,0:T(8,128)S(1)}, f32[3,8,256]{2,1,0:T(8,128)S(1)}, u32[]{:S(2)}, u32[]{:S(2)}) collective-permute-start(f32[3,8,256]{2,1,0:T(8,128)S(1)} %get-tuple-element.372), channel_id=1, source_target_pairs={{0,1},{1,2},{2,3},{3,4},{4,5},{5,6},{6,7},{7,0},{8,9},{9,10},{10,1... | collective-permute-start | bytes 73736 | tf_op jit(solution)/shard_map/ppermute | solution.py:19
  28.8 1.6 %collective-permute-start.8 = (f32[3,8,256]{2,1,0:T(8,128)S(1)}, f32[3,8,256]{2,1,0:T(8,128)S(1)}, u32[]{:S(2)}, u32[]{:S(2)}) collective-permute-start(f32[3,8,256]{2,1,0:T(8,128)S(1)} %get-tuple-element.371), channel_id=1, source_target_pairs={{1,0},{2,1},{3,2},{4,3},{5,4},{6,5},{7,6},{0,7},{9,8},{10,9},{11,1... | collective-permute-start | bytes 73736 | tf_op jit(solution)/shard_map/ppermute | solution.py:22
  28.9 5.1 %collective-permute-start.7 = (f32[3,8,256]{2,1,0:T(8,128)S(1)}, f32[3,8,256]{2,1,0:T(8,128)S(1)}, u32[]{:S(2)}, u32[]{:S(2)}) collective-permute-start(f32[3,8,256]{2,1,0:T(8,128)S(1)} %get-tuple-element.370), channel_id=1, source_target_pairs={{0,1},{1,2},{2,3},{3,4},{4,5},{5,6},{6,7},{7,0},{8,9},{9,10},{10,1... | collective-permute-start | bytes 73736 | tf_op jit(solution)/shard_map/ppermute | solution.py:19
  42.0 7.1 %collective-permute-start.9 = (f32[3,24,256]{2,1,0:T(8,128)S(1)}, f32[3,24,256]{2,1,0:T(8,128)S(1)}, u32[]{:S(2)}, u32[]{:S(2)}) collective-permute-start(f32[3,24,256]{2,1,0:T(8,128)S(1)} %fusion.57), channel_id=1, source_target_pairs={{0,8},{8,16},{16,24},{1,9},{9,17},{17,25},{2,10},{10,18},{18,26},{... | collective-permute-start | bytes 221192 | tf_op jit(solution)/shard_map/ppermute | solution.py:30
  49.2 1.6 %collective-permute-start.11 = (f32[3,8,256]{2,1,0:T(8,128)S(1)}, f32[3,8,256]{2,1,0:T(8,128)S(1)}, u32[]{:S(2)}, u32[]{:S(2)}) collective-permute-start(f32[3,8,256]{2,1,0:T(8,128)S(1)} %get-tuple-element.369), channel_id=1, source_target_pairs={{1,0},{2,1},{3,2},{4,3},{5,4},{6,5},{7,6},{0,7},{9,8},{10,9},{11,1... | collective-permute-start | bytes 73736 | tf_op jit(solution)/shard_map/ppermute | solution.py:22
  49.3 5.1 %collective-permute-start.10 = (f32[3,8,256]{2,1,0:T(8,128)S(1)}, f32[3,8,256]{2,1,0:T(8,128)S(1)}, u32[]{:S(2)}, u32[]{:S(2)}) collective-permute-start(f32[3,8,256]{2,1,0:T(8,128)S(1)} %get-tuple-element.368), channel_id=1, source_target_pairs={{0,1},{1,2},{2,3},{3,4},{4,5},{5,6},{6,7},{7,0},{8,9},{9,10},{10,1... | collective-permute-start | bytes 73736 | tf_op jit(solution)/shard_map/ppermute | solution.py:19
  63.1 1.6 %collective-permute-start.13 = (f32[3,8,256]{2,1,0:T(8,128)S(1)}, f32[3,8,256]{2,1,0:T(8,128)S(1)}, u32[]{:S(2)}, u32[]{:S(2)}) collective-permute-start(f32[3,8,256]{2,1,0:T(8,128)S(1)} %get-tuple-element.367), channel_id=1, source_target_pairs={{1,0},{2,1},{3,2},{4,3},{5,4},{6,5},{7,6},{0,7},{9,8},{10,9},{11,1... | collective-permute-start | bytes 73736 | tf_op jit(solution)/shard_map/ppermute | solution.py:22
  63.2 5.3 %collective-permute-start.12 = (f32[3,8,256]{2,1,0:T(8,128)S(1)}, f32[3,8,256]{2,1,0:T(8,128)S(1)}, u32[]{:S(2)}, u32[]{:S(2)}) collective-permute-start(f32[3,8,256]{2,1,0:T(8,128)S(1)} %get-tuple-element.366), channel_id=1, source_target_pairs={{0,1},{1,2},{2,3},{3,4},{4,5},{5,6},{6,7},{7,0},{8,9},{9,10},{10,1... | collective-permute-start | bytes 73736 | tf_op jit(solution)/shard_map/ppermute | solution.py:19
  76.5 1.6 %collective-permute-start.15 = (f32[3,8,256]{2,1,0:T(8,128)S(1)}, f32[3,8,256]{2,1,0:T(8,128)S(1)}, u32[]{:S(2)}, u32[]{:S(2)}) collective-permute-start(f32[3,8,256]{2,1,0:T(8,128)S(1)} %get-tuple-element.365), channel_id=1, source_target_pairs={{1,0},{2,1},{3,2},{4,3},{5,4},{6,5},{7,6},{0,7},{9,8},{10,9},{11,1... | collective-permute-start | bytes 73736 | tf_op jit(solution)/shard_map/ppermute | solution.py:22
  76.6 5.1 %collective-permute-start.14 = (f32[3,8,256]{2,1,0:T(8,128)S(1)}, f32[3,8,256]{2,1,0:T(8,128)S(1)}, u32[]{:S(2)}, u32[]{:S(2)}) collective-permute-start(f32[3,8,256]{2,1,0:T(8,128)S(1)} %get-tuple-element.364), channel_id=1, source_target_pairs={{0,1},{1,2},{2,3},{3,4},{4,5},{5,6},{6,7},{7,0},{8,9},{9,10},{10,1... | collective-permute-start | bytes 73736 | tf_op jit(solution)/shard_map/ppermute | solution.py:19
  96.5 7.2 %copy-start.2 = (f32[3,24,256]{2,1,0:T(8,128)}, f32[3,24,256]{2,1,0:T(8,128)S(1)}, u32[]{:S(2)}) copy-start(f32[3,24,256]{2,1,0:T(8,128)S(1)} %fusion.47) | copy-start | bytes 221188
  96.5 7.1 %collective-permute-start.16 = (f32[3,24,256]{2,1,0:T(8,128)S(1)}, f32[3,24,256]{2,1,0:T(8,128)S(1)}, u32[]{:S(2)}, u32[]{:S(2)}) collective-permute-start(f32[3,24,256]{2,1,0:T(8,128)S(1)} %fusion.47), channel_id=1, source_target_pairs={{0,8},{8,16},{16,24},{1,9},{9,17},{17,25},{2,10},{10,18},{18,26},{... | collective-permute-start | bytes 221192 | tf_op jit(solution)/shard_map/ppermute | solution.py:30
  103.7 1.6 %collective-permute-start.18 = (f32[3,8,256]{2,1,0:T(8,128)S(1)}, f32[3,8,256]{2,1,0:T(8,128)S(1)}, u32[]{:S(2)}, u32[]{:S(2)}) collective-permute-start(f32[3,8,256]{2,1,0:T(8,128)S(1)} %get-tuple-element.359), channel_id=1, source_target_pairs={{1,0},{2,1},{3,2},{4,3},{5,4},{6,5},{7,6},{0,7},{9,8},{10,9},{11,1... | collective-permute-start | bytes 73736 | tf_op jit(solution)/shard_map/ppermute | solution.py:22
  103.7 5.1 %collective-permute-start.17 = (f32[3,8,256]{2,1,0:T(8,128)S(1)}, f32[3,8,256]{2,1,0:T(8,128)S(1)}, u32[]{:S(2)}, u32[]{:S(2)}) collective-permute-start(f32[3,8,256]{2,1,0:T(8,128)S(1)} %get-tuple-element.358), channel_id=1, source_target_pairs={{0,1},{1,2},{2,3},{3,4},{4,5},{5,6},{6,7},{7,0},{8,9},{9,10},{10,1... | collective-permute-start | bytes 73736 | tf_op jit(solution)/shard_map/ppermute | solution.py:19
  116.9 1.6 %collective-permute-start.20 = (f32[3,6,256]{2,1,0:T(8,128)S(1)}, f32[3,6,256]{2,1,0:T(8,128)S(1)}, u32[]{:S(2)}, u32[]{:S(2)}) collective-permute-start(f32[3,6,256]{2,1,0:T(8,128)S(1)} %get-tuple-element.357), channel_id=1, source_target_pairs={{1,0},{2,1},{3,2},{4,3},{5,4},{6,5},{7,6},{0,7},{9,8},{10,9},{11,1... | collective-permute-start | bytes 55304 | tf_op jit(solution)/shard_map/ppermute | solution.py:22
  117.0 5.1 %collective-permute-start.19 = (f32[3,6,256]{2,1,0:T(8,128)S(1)}, f32[3,6,256]{2,1,0:T(8,128)S(1)}, u32[]{:S(2)}, u32[]{:S(2)}) collective-permute-start(f32[3,6,256]{2,1,0:T(8,128)S(1)} %get-tuple-element.356), channel_id=1, source_target_pairs={{0,1},{1,2},{2,3},{3,4},{4,5},{5,6},{6,7},{7,0},{8,9},{9,10},{10,1... | collective-permute-start | bytes 55304 | tf_op jit(solution)/shard_map/ppermute | solution.py:19
where the time goes:
time: 129 us
  waiting for transfers between devices  41.9 us (32%)
  local copies, waits for them, and re-layouts  34.5 us (27%)
  other arithmetic  20.8 us (16%)
  starting transfers between devices  20 us (16%)
  blocking collectives  8.68 us (7%)
  between operations  2.78 us (2%)
    ppermute x9, waiting for transfers between devices, with_halo(): lax.ppermute(lax.slice_in_dim(block, block.shape[dim] - width, None, axis...  25.2 us
    slice x326, local copies, waits for them, and re-layouts, cut_neighbours(): jnp.roll(field, 1, 1)[1:-1]  24.3 us
    another operation x165, other arithmetic, tendency(): return jnp.stack([rate_height, rate_row, rate_col])  17.3 us
    ppermute x3, waiting for transfers between devices, shifted(): return lax.ppermute(value, axis, pairs)  9.3 us
    ppermute x3, starting transfers between devices, shifted(): return lax.ppermute(value, axis, pairs)  8.96 us
    all_gather x1, blocking collectives, body(): gathered = lax.all_gather(defect_pad[None], 'tm', axis=0, tiled=True)  8.68 us
    slice x110, local copies, waits for them, and re-layouts, cut_neighbours(): jnp.roll(field, -1, 1)[1:-1]  8.11 us
    ppermute x9, waiting for transfers between devices, with_halo(): lax.ppermute(lax.slice_in_dim(block, 0, width, axis=dim), axis, backward)  7.4 us
  transfers between devices with their start and end apart: 21, of which 19 were waited for; matrix products, arithmetic and copies ran while one was open for 1% of the time, Pallas kernels for 0%

commit v1 on v0

--- a/solution.py
+++ b/solution.py
@@ -123,7 +123,12 @@
     fine_end, coarse_end = advance(earlier(relaxed), drag_pad, STEPS, layers, True)
     defect = fine_end - coarse_end
     defect_pad = with_halo(defect, (("space", 1),), 8)
-    gathered = lax.all_gather(defect_pad[None], "tm", axis=0, tiled=True)
+    ring = [defect_pad[None]]
+    for hop in range(3):
+        ring.append(lax.ppermute(ring[-1], "tm", [(dev, (dev + 1) % 4) for dev in range(4)]))
+    gathered = jnp.roll(
+        jnp.concatenate(ring[::-1], axis=0), (lax.axis_index("tm") + 1) * ring[0].shape[0], axis=0
+    )
 
     def group_fn(group, carry):
         current, owned = carry

time: 129 us -> 139 us (1.078)
  waiting for transfers between devices: 41.9 us -> 61.6 us
  blocking collectives: 8.68 us -> 0 us
  starting transfers between devices: 20 us -> 18.3 us
    ppermute x0 -> x3, waiting for transfers between devices: none -> 18.5 us  [body(): lax.ppermute(ring[-1], 'tm', [(dev, (dev + 1) % 4) for dev in range(4)])]
    all_gather x1 -> x0, blocking collectives: 8.68 us -> none  [body(): gathered = lax.all_gather(defect_pad[None], 'tm', axis=0, tiled=True)]
    ppermute x3, starting transfers between devices: 8.96 us -> 7.23 us  [shifted(): return lax.ppermute(value, axis, pairs)]
    ppermute x3, waiting for transfers between devices: 9.3 us -> 10.9 us  [shifted(): return lax.ppermute(value, axis, pairs)]
  transfers between devices with their start and end apart: 21 -> 24, of which waited for: 19 -> 21; matrix products, arithmetic and copies ran while one was open for 1% -> 1% of each run, Pallas kernels for 0% -> 0%
where the time goes in v1:
time: 139 us
  waiting for transfers between devices  61.6 us (44%)
  local copies, waits for them, and re-layouts  35.4 us (25%)
  other arithmetic  20.8 us (15%)
  starting transfers between devices  18.3 us (13%)
  between operations  2.84 us (2%)
    ppermute x9, waiting for transfers between devices, with_halo(): lax.ppermute(lax.slice_in_dim(block, block.shape[dim] - width, None, axis...  25.2 us
    slice x326, local copies, waits for them, and re-layouts, cut_neighbours(): jnp.roll(field, 1, 1)[1:-1]  24.3 us
    ppermute x3, waiting for transfers between devices, body(): lax.ppermute(ring[-1], 'tm', [(dev, (dev + 1) % 4) for dev in range(4)])  18.5 us
    another operation x165, other arithmetic, tendency(): return jnp.stack([rate_height, rate_row, rate_col])  17.3 us
    ppermute x3, waiting for transfers between devices, shifted(): return lax.ppermute(value, axis, pairs)  10.9 us
    slice x110, local copies, waits for them, and re-layouts, cut_neighbours(): jnp.roll(field, -1, 1)[1:-1]  8.11 us
    ppermute x3, starting transfers between devices, shifted(): return lax.ppermute(value, axis, pairs)  7.23 us
    ppermute x9, waiting for transfers between devices, with_halo(): lax.ppermute(lax.slice_in_dim(block, 0, width, axis=dim), axis, backward)  6.97 us
  transfers between devices with their start and end apart: 24, of which 21 were waited for; matrix products, arithmetic and copies ran while one was open for 1% of the time, Pallas kernels for 0%

profile of v1, /device:TPU:4, one launch (start us, length us, event | category | flops | bytes accessed | tf_op | source)
XLA Modules:
  0.0 139.0 jit_solution(15917465170785556836)
XLA Ops:
  0.6 0.8 fusion.2103
  1.4 0.8 fusion.1657
  2.2 1.7 %collective-permute-start = (f32[3,8,256]{2,1,0:T(8,128)S(1)}, f32[3,8,256]{2,1,0:T(8,128)S(1)}, u32[]{:S(2)}, u32[]{:S(2)}) collective-permute-start(f32[3,8,256]{2,1,0:T(8,128)S(1)} %get-tuple-element.365), channel_id=1, source_target_pairs={{0,1},{1,2},{2,3},{3,4},{4,5},{5,6},{6,7},{7,0},{8,9},{9,10},{10,1... | collective-permute-start | bytes 73736 | tf_op jit(solution)/shard_map/while/body/eval_jaxpr/ppermute | solution.py:19
  3.8 3.4 %collective-permute-start.4 = (f32[3,24,256]{2,1,0:T(8,128)S(1)}, f32[3,24,256]{2,1,0:T(8,128)S(1)}, u32[]{:S(2)}, u32[]{:S(2)}) collective-permute-start(f32[3,24,256]{2,1,0:T(8,128)S(1)} %bitcast.5629), channel_id=1, source_target_pairs={{0,8},{8,16},{16,24},{1,9},{9,17},{17,25},{2,10},{10,18},{18,26},{... | collective-permute-start | bytes 221192 | tf_op jit(solution)/shard_map/ppermute | solution.py:30
  7.2 1.6 %collective-permute-start.3 = (f32[8,256]{1,0:T(8,128)S(1)}, f32[8,256]{1,0:T(8,128)S(1)}, u32[]{:S(2)}, u32[]{:S(2)}) collective-permute-start(f32[8,256]{1,0:T(8,128)S(1)} %get-tuple-element.1258), channel_id=1, source_target_pairs={{1,0},{2,1},{3,2},{4,3},{5,4},{6,5},{7,6},{0,7},{9,8},{10,9},{11,1... | collective-permute-start | bytes 24584 | tf_op jit(solution)/shard_map/ppermute | solution.py:22
  8.9 0.8 collective-permute-start.1
  9.7 0.7 copy-done
  10.4 0.6 collective-permute-done.4
  11.0 0.2 collective-permute-done.1
  12.1 3.6 %collective-permute-start.6 = (f32[3,8,256]{2,1,0:T(8,128)S(1)}, f32[3,8,256]{2,1,0:T(8,128)S(1)}, u32[]{:S(2)}, u32[]{:S(2)}) collective-permute-start(f32[3,8,256]{2,1,0:T(8,128)S(1)} %get-tuple-element.377), channel_id=1, source_target_pairs={{1,0},{2,1},{3,2},{4,3},{5,4},{6,5},{7,6},{0,7},{9,8},{10,9},{11,1... | collective-permute-start | bytes 73736 | tf_op jit(solution)/shard_map/ppermute | solution.py:22
  16.0 1.2 collective-permute-done.6
  17.2 3.5 %collective-permute-done.5 = f32[3,8,256]{2,1,0:T(8,128)S(1)} collective-permute-done((f32[3,8,256]{2,1,0:T(8,128)S(1)}, f32[3,8,256]{2,1,0:T(8,128)S(1)}, u32[]{:S(2)}, u32[]{:S(2)}) %collective-permute-start.5) | collective-permute-done | bytes 24608 | tf_op jit(solution)/shard_map/ppermute | solution.py:19
  21.4 0.1 fusion.584
  22.4 0.1 fusion.564
  23.5 0.1 fusion.544
  28.7 0.5 collective-permute-start.7
  29.3 0.9 collective-permute-done.8
  30.2 3.6 %collective-permute-done.7 = f32[3,8,256]{2,1,0:T(8,128)S(1)} collective-permute-done((f32[3,8,256]{2,1,0:T(8,128)S(1)}, f32[3,8,256]{2,1,0:T(8,128)S(1)}, u32[]{:S(2)}, u32[]{:S(2)}) %collective-permute-start.7) | collective-permute-done | bytes 24608 | tf_op jit(solution)/shard_map/ppermute | solution.py:19
  34.6 0.1 fusion.524
  35.6 0.1 fusion.504
  41.9 1.9 %collective-permute-start.9 = (f32[3,24,256]{2,1,0:T(8,128)S(1)}, f32[3,24,256]{2,1,0:T(8,128)S(1)}, u32[]{:S(2)}, u32[]{:S(2)}) collective-permute-start(f32[3,24,256]{2,1,0:T(8,128)S(1)} %fusion.57), channel_id=1, source_target_pairs={{0,8},{8,16},{16,24},{1,9},{9,17},{17,25},{2,10},{10,18},{18,26},{... | collective-permute-start | bytes 221192 | tf_op jit(solution)/shard_map/ppermute | solution.py:30
  43.9 5.1 %collective-permute-done.9 = f32[3,24,256]{2,1,0:T(8,128)S(1)} collective-permute-done((f32[3,24,256]{2,1,0:T(8,128)S(1)}, f32[3,24,256]{2,1,0:T(8,128)S(1)}, u32[]{:S(2)}, u32[]{:S(2)}) %collective-permute-start.9) | collective-permute-done | bytes 73760 | tf_op jit(solution)/shard_map/ppermute | solution.py:30
  49.1 0.5 collective-permute-start.10
  49.7 0.9 collective-permute-done.11
  50.6 3.6 %collective-permute-done.10 = f32[3,8,256]{2,1,0:T(8,128)S(1)} collective-permute-done((f32[3,8,256]{2,1,0:T(8,128)S(1)}, f32[3,8,256]{2,1,0:T(8,128)S(1)}, u32[]{:S(2)}, u32[]{:S(2)}) %collective-permute-start.10) | collective-permute-done | bytes 24608 | tf_op jit(solution)/shard_map/ppermute | solution.py:19
  56.7 0.1 fusion.444
  57.7 0.1 fusion.424
  63.0 0.5 collective-permute-start.12
  63.6 0.1 fusion.344
  63.8 0.7 collective-permute-done.13
  64.5 3.7 %collective-permute-done.12 = f32[3,8,256]{2,1,0:T(8,128)S(1)} collective-permute-done((f32[3,8,256]{2,1,0:T(8,128)S(1)}, f32[3,8,256]{2,1,0:T(8,128)S(1)}, u32[]{:S(2)}, u32[]{:S(2)}) %collective-permute-start.12) | collective-permute-done | bytes 24608 | tf_op jit(solution)/shard_map/ppermute | solution.py:19
  71.1 0.1 fusion.364
  76.4 0.5 collective-permute-start.14
  77.0 0.9 collective-permute-done.15
  78.0 3.6 %collective-permute-done.14 = f32[3,8,256]{2,1,0:T(8,128)S(1)} collective-permute-done((f32[3,8,256]{2,1,0:T(8,128)S(1)}, f32[3,8,256]{2,1,0:T(8,128)S(1)}, u32[]{:S(2)}, u32[]{:S(2)}) %collective-permute-start.14) | collective-permute-done | bytes 24608 | tf_op jit(solution)/shard_map/ppermute | solution.py:19
  81.7 6.7 %collective-permute-done.16 = f32[1,3,40,256]{3,2,1,0:T(8,128)S(1)} collective-permute-done((f32[1,3,40,256]{3,2,1,0:T(8,128)S(1)}, f32[1,3,40,256]{3,2,1,0:T(8,128)S(1)}, u32[]{:S(2)}, u32[]{:S(2)}) %collective-permute-start.16) | collective-permute-done | bytes 122912 | tf_op jit(solution)/shard_map/ppermute | solution.py:128
  88.5 6.2 %collective-permute-done.17 = f32[1,3,40,256]{3,2,1,0:T(8,128)S(1)} collective-permute-done((f32[1,3,40,256]{3,2,1,0:T(8,128)S(1)}, f32[1,3,40,256]{3,2,1,0:T(8,128)S(1)}, u32[]{:S(2)}, u32[]{:S(2)}) %collective-permute-start.17) | collective-permute-done | bytes 122912 | tf_op jit(solution)/shard_map/ppermute | solution.py:128
  94.8 5.7 %collective-permute-done.18 = f32[1,3,40,256]{3,2,1,0:T(8,128)S(1)} collective-permute-done((f32[1,3,40,256]{3,2,1,0:T(8,128)S(1)}, f32[1,3,40,256]{3,2,1,0:T(8,128)S(1)}, u32[]{:S(2)}, u32[]{:S(2)}) %collective-permute-start.18) | collective-permute-done | bytes 122912 | tf_op jit(solution)/shard_map/ppermute | solution.py:128
  106.8 1.9 %collective-permute-start.19 = (f32[3,24,256]{2,1,0:T(8,128)S(1)}, f32[3,24,256]{2,1,0:T(8,128)S(1)}, u32[]{:S(2)}, u32[]{:S(2)}) collective-permute-start(f32[3,24,256]{2,1,0:T(8,128)S(1)} %fusion.47), channel_id=1, source_target_pairs={{0,8},{8,16},{16,24},{1,9},{9,17},{17,25},{2,10},{10,18},{18,26},{... | collective-permute-start | bytes 221192 | tf_op jit(solution)/shard_map/ppermute | solution.py:30
  108.7 5.2 %collective-permute-done.19 = f32[3,24,256]{2,1,0:T(8,128)S(1)} collective-permute-done((f32[3,24,256]{2,1,0:T(8,128)S(1)}, f32[3,24,256]{2,1,0:T(8,128)S(1)}, u32[]{:S(2)}, u32[]{:S(2)}) %collective-permute-start.19) | collective-permute-done | bytes 73760 | tf_op jit(solution)/shard_map/ppermute | solution.py:30
  114.0 0.5 collective-permute-start.20
  114.5 1.0 collective-permute-done.21
  115.5 3.6 %collective-permute-done.20 = f32[3,8,256]{2,1,0:T(8,128)S(1)} collective-permute-done((f32[3,8,256]{2,1,0:T(8,128)S(1)}, f32[3,8,256]{2,1,0:T(8,128)S(1)}, u32[]{:S(2)}, u32[]{:S(2)}) %collective-permute-start.20) | collective-permute-done | bytes 24608 | tf_op jit(solution)/shard_map/ppermute | solution.py:19
  120.9 0.1 fusion.284
  127.3 0.5 collective-permute-start.22
  127.8 1.0 collective-permute-done.23
  128.8 3.6 %collective-permute-done.22 = f32[3,6,256]{2,1,0:T(8,128)S(1)} collective-permute-done((f32[3,6,256]{2,1,0:T(8,128)S(1)}, f32[3,6,256]{2,1,0:T(8,128)S(1)}, u32[]{:S(2)}, u32[]{:S(2)}) %collective-permute-start.22) | collective-permute-done | bytes 18464 | tf_op jit(solution)/shard_map/ppermute | solution.py:19
  138.3 0.7 fusion.42
  (806 shorter events, 52.6 us)
Async XLA Ops:
  0.6 3.2 %copy-start.3 = (f32[1,3,24,256]{3,2,1,0:T(8,128)S(1)}, f32[1,3,24,256]{3,2,1,0:T(8,128)}, u32[]{:S(2)}) copy-start(f32[1,3,24,256]{3,2,1,0:T(8,128)} %param.4) | copy-start | bytes 221188
  1.4 8.3 %collective-permute-start.2 = (f32[8,256]{1,0:T(8,128)S(1)}, f32[8,256]{1,0:T(8,128)S(1)}, u32[]{:S(2)}, u32[]{:S(2)}) collective-permute-start(f32[8,256]{1,0:T(8,128)S(1)} %get-tuple-element.1259), channel_id=1, source_target_pairs={{0,1},{1,2},{2,3},{3,4},{4,5},{5,6},{6,7},{7,0},{8,9},{9,10},{10,1... | collective-permute-start | bytes 24584 | tf_op jit(solution)/shard_map/ppermute | solution.py:19
  2.2 8.3 %collective-permute-start = (f32[3,8,256]{2,1,0:T(8,128)S(1)}, f32[3,8,256]{2,1,0:T(8,128)S(1)}, u32[]{:S(2)}, u32[]{:S(2)}) collective-permute-start(f32[3,8,256]{2,1,0:T(8,128)S(1)} %get-tuple-element.365), channel_id=1, source_target_pairs={{0,1},{1,2},{2,3},{3,4},{4,5},{5,6},{6,7},{7,0},{8,9},{9,10},{10,1... | collective-permute-start | bytes 73736 | tf_op jit(solution)/shard_map/while/body/eval_jaxpr/ppermute | solution.py:19
  3.8 7.1 %collective-permute-start.4 = (f32[3,24,256]{2,1,0:T(8,128)S(1)}, f32[3,24,256]{2,1,0:T(8,128)S(1)}, u32[]{:S(2)}, u32[]{:S(2)}) collective-permute-start(f32[3,24,256]{2,1,0:T(8,128)S(1)} %bitcast.5629), channel_id=1, source_target_pairs={{0,8},{8,16},{16,24},{1,9},{9,17},{17,25},{2,10},{10,18},{18,26},{... | collective-permute-start | bytes 221192 | tf_op jit(solution)/shard_map/ppermute | solution.py:30
  7.2 3.2 %collective-permute-start.3 = (f32[8,256]{1,0:T(8,128)S(1)}, f32[8,256]{1,0:T(8,128)S(1)}, u32[]{:S(2)}, u32[]{:S(2)}) collective-permute-start(f32[8,256]{1,0:T(8,128)S(1)} %get-tuple-element.1258), channel_id=1, source_target_pairs={{1,0},{2,1},{3,2},{4,3},{5,4},{6,5},{7,6},{0,7},{9,8},{10,9},{11,1... | collective-permute-start | bytes 24584 | tf_op jit(solution)/shard_map/ppermute | solution.py:22
  8.9 2.3 %collective-permute-start.1 = (f32[3,8,256]{2,1,0:T(8,128)S(1)}, f32[3,8,256]{2,1,0:T(8,128)S(1)}, u32[]{:S(2)}, u32[]{:S(2)}) collective-permute-start(f32[3,8,256]{2,1,0:T(8,128)S(1)} %get-tuple-element.364), channel_id=1, source_target_pairs={{1,0},{2,1},{3,2},{4,3},{5,4},{6,5},{7,6},{0,7},{9,8},{10,9},{11,1... | collective-permute-start | bytes 73736 | tf_op jit(solution)/shard_map/while/body/eval_jaxpr/ppermute | solution.py:22
  9.7 0.7 copy-start
  9.7 1.3 copy-start.1
  12.1 5.1 %collective-permute-start.6 = (f32[3,8,256]{2,1,0:T(8,128)S(1)}, f32[3,8,256]{2,1,0:T(8,128)S(1)}, u32[]{:S(2)}, u32[]{:S(2)}) collective-permute-start(f32[3,8,256]{2,1,0:T(8,128)S(1)} %get-tuple-element.377), channel_id=1, source_target_pairs={{1,0},{2,1},{3,2},{4,3},{5,4},{6,5},{7,6},{0,7},{9,8},{10,9},{11,1... | collective-permute-start | bytes 73736 | tf_op jit(solution)/shard_map/ppermute | solution.py:22
  15.7 5.0 %collective-permute-start.5 = (f32[3,8,256]{2,1,0:T(8,128)S(1)}, f32[3,8,256]{2,1,0:T(8,128)S(1)}, u32[]{:S(2)}, u32[]{:S(2)}) collective-permute-start(f32[3,8,256]{2,1,0:T(8,128)S(1)} %get-tuple-element.376), channel_id=1, source_target_pairs={{0,1},{1,2},{2,3},{3,4},{4,5},{5,6},{6,7},{7,0},{8,9},{9,10},{10,1... | collective-permute-start | bytes 73736 | tf_op jit(solution)/shard_map/ppermute | solution.py:19
  28.7 1.6 %collective-permute-start.8 = (f32[3,8,256]{2,1,0:T(8,128)S(1)}, f32[3,8,256]{2,1,0:T(8,128)S(1)}, u32[]{:S(2)}, u32[]{:S(2)}) collective-permute-start(f32[3,8,256]{2,1,0:T(8,128)S(1)} %get-tuple-element.375), channel_id=1, source_target_pairs={{1,0},{2,1},{3,2},{4,3},{5,4},{6,5},{7,6},{0,7},{9,8},{10,9},{11,1... | collective-permute-start | bytes 73736 | tf_op jit(solution)/shard_map/ppermute | solution.py:22
  28.7 5.1 %collective-permute-start.7 = (f32[3,8,256]{2,1,0:T(8,128)S(1)}, f32[3,8,256]{2,1,0:T(8,128)S(1)}, u32[]{:S(2)}, u32[]{:S(2)}) collective-permute-start(f32[3,8,256]{2,1,0:T(8,128)S(1)} %get-tuple-element.374), channel_id=1, source_target_pairs={{0,1},{1,2},{2,3},{3,4},{4,5},{5,6},{6,7},{7,0},{8,9},{9,10},{10,1... | collective-permute-start | bytes 73736 | tf_op jit(solution)/shard_map/ppermute | solution.py:19
  41.9 7.1 %collective-permute-start.9 = (f32[3,24,256]{2,1,0:T(8,128)S(1)}, f32[3,24,256]{2,1,0:T(8,128)S(1)}, u32[]{:S(2)}, u32[]{:S(2)}) collective-permute-start(f32[3,24,256]{2,1,0:T(8,128)S(1)} %fusion.57), channel_id=1, source_target_pairs={{0,8},{8,16},{16,24},{1,9},{9,17},{17,25},{2,10},{10,18},{18,26},{... | collective-permute-start | bytes 221192 | tf_op jit(solution)/shard_map/ppermute | solution.py:30
  49.1 1.6 %collective-permute-start.11 = (f32[3,8,256]{2,1,0:T(8,128)S(1)}, f32[3,8,256]{2,1,0:T(8,128)S(1)}, u32[]{:S(2)}, u32[]{:S(2)}) collective-permute-start(f32[3,8,256]{2,1,0:T(8,128)S(1)} %get-tuple-element.373), channel_id=1, source_target_pairs={{1,0},{2,1},{3,2},{4,3},{5,4},{6,5},{7,6},{0,7},{9,8},{10,9},{11,1... | collective-permute-start | bytes 73736 | tf_op jit(solution)/shard_map/ppermute | solution.py:22
  49.1 5.1 %collective-permute-start.10 = (f32[3,8,256]{2,1,0:T(8,128)S(1)}, f32[3,8,256]{2,1,0:T(8,128)S(1)}, u32[]{:S(2)}, u32[]{:S(2)}) collective-permute-start(f32[3,8,256]{2,1,0:T(8,128)S(1)} %get-tuple-element.372), channel_id=1, source_target_pairs={{0,1},{1,2},{2,3},{3,4},{4,5},{5,6},{6,7},{7,0},{8,9},{9,10},{10,1... | collective-permute-start | bytes 73736 | tf_op jit(solution)/shard_map/ppermute | solution.py:19
  62.9 1.6 %collective-permute-start.13 = (f32[3,8,256]{2,1,0:T(8,128)S(1)}, f32[3,8,256]{2,1,0:T(8,128)S(1)}, u32[]{:S(2)}, u32[]{:S(2)}) collective-permute-start(f32[3,8,256]{2,1,0:T(8,128)S(1)} %get-tuple-element.371), channel_id=1, source_target_pairs={{1,0},{2,1},{3,2},{4,3},{5,4},{6,5},{7,6},{0,7},{9,8},{10,9},{11,1... | collective-permute-start | bytes 73736 | tf_op jit(solution)/shard_map/ppermute | solution.py:22
  63.0 5.3 %collective-permute-start.12 = (f32[3,8,256]{2,1,0:T(8,128)S(1)}, f32[3,8,256]{2,1,0:T(8,128)S(1)}, u32[]{:S(2)}, u32[]{:S(2)}) collective-permute-start(f32[3,8,256]{2,1,0:T(8,128)S(1)} %get-tuple-element.370), channel_id=1, source_target_pairs={{0,1},{1,2},{2,3},{3,4},{4,5},{5,6},{6,7},{7,0},{8,9},{9,10},{10,1... | collective-permute-start | bytes 73736 | tf_op jit(solution)/shard_map/ppermute | solution.py:19
  76.4 1.6 %collective-permute-start.15 = (f32[3,8,256]{2,1,0:T(8,128)S(1)}, f32[3,8,256]{2,1,0:T(8,128)S(1)}, u32[]{:S(2)}, u32[]{:S(2)}) collective-permute-start(f32[3,8,256]{2,1,0:T(8,128)S(1)} %get-tuple-element.369), channel_id=1, source_target_pairs={{1,0},{2,1},{3,2},{4,3},{5,4},{6,5},{7,6},{0,7},{9,8},{10,9},{11,1... | collective-permute-start | bytes 73736 | tf_op jit(solution)/shard_map/ppermute | solution.py:22
  76.4 5.1 %collective-permute-start.14 = (f32[3,8,256]{2,1,0:T(8,128)S(1)}, f32[3,8,256]{2,1,0:T(8,128)S(1)}, u32[]{:S(2)}, u32[]{:S(2)}) collective-permute-start(f32[3,8,256]{2,1,0:T(8,128)S(1)} %get-tuple-element.368), channel_id=1, source_target_pairs={{0,1},{1,2},{2,3},{3,4},{4,5},{5,6},{6,7},{7,0},{8,9},{9,10},{10,1... | collective-permute-start | bytes 73736 | tf_op jit(solution)/shard_map/ppermute | solution.py:19
  81.6 6.9 %collective-permute-start.16 = (f32[1,3,40,256]{3,2,1,0:T(8,128)S(1)}, f32[1,3,40,256]{3,2,1,0:T(8,128)S(1)}, u32[]{:S(2)}, u32[]{:S(2)}) collective-permute-start(f32[1,3,40,256]{3,2,1,0:T(8,128)S(1)} %maximum_bitcast_fusion), channel_id=1, source_target_pairs={{0,8},{8,16},{16,24},{24,0},{1,9},{9,17},{17,25},{25,1},{2,10},{10... | collective-permute-start | bytes 368648 | tf_op jit(solution)/shard_map/ppermute | solution.py:128
  88.5 6.2 %collective-permute-start.17 = (f32[1,3,40,256]{3,2,1,0:T(8,128)S(1)}, f32[1,3,40,256]{3,2,1,0:T(8,128)S(1)}, u32[]{:S(2)}, u32[]{:S(2)}) collective-permute-start(f32[1,3,40,256]{3,2,1,0:T(8,128)S(1)} %collective-permute-done.16), channel_id=1, source_target_pairs={{0,8},{8,16},{16,24},{24,0},{1,9},{9,17},{17,25},{25,1},{2,10},{10... | collective-permute-start | bytes 368648 | tf_op jit(solution)/shard_map/ppermute | solution.py:128
  94.7 5.8 %collective-permute-start.18 = (f32[1,3,40,256]{3,2,1,0:T(8,128)S(1)}, f32[1,3,40,256]{3,2,1,0:T(8,128)S(1)}, u32[]{:S(2)}, u32[]{:S(2)}) collective-permute-start(f32[1,3,40,256]{3,2,1,0:T(8,128)S(1)} %collective-permute-done.17), channel_id=1, source_target_pairs={{0,8},{8,16},{16,24},{24,0},{1,9},{9,17},{17,25},{25,1},{2,10},{10... | collective-permute-start | bytes 368648 | tf_op jit(solution)/shard_map/ppermute | solution.py:128
  106.8 7.2 %copy-start.2 = (f32[3,24,256]{2,1,0:T(8,128)}, f32[3,24,256]{2,1,0:T(8,128)S(1)}, u32[]{:S(2)}) copy-start(f32[3,24,256]{2,1,0:T(8,128)S(1)} %fusion.47) | copy-start | bytes 221188
  106.8 7.1 %collective-permute-start.19 = (f32[3,24,256]{2,1,0:T(8,128)S(1)}, f32[3,24,256]{2,1,0:T(8,128)S(1)}, u32[]{:S(2)}, u32[]{:S(2)}) collective-permute-start(f32[3,24,256]{2,1,0:T(8,128)S(1)} %fusion.47), channel_id=1, source_target_pairs={{0,8},{8,16},{16,24},{1,9},{9,17},{17,25},{2,10},{10,18},{18,26},{... | collective-permute-start | bytes 221192 | tf_op jit(solution)/shard_map/ppermute | solution.py:30
  114.0 1.6 %collective-permute-start.21 = (f32[3,8,256]{2,1,0:T(8,128)S(1)}, f32[3,8,256]{2,1,0:T(8,128)S(1)}, u32[]{:S(2)}, u32[]{:S(2)}) collective-permute-start(f32[3,8,256]{2,1,0:T(8,128)S(1)} %get-tuple-element.363), channel_id=1, source_target_pairs={{1,0},{2,1},{3,2},{4,3},{5,4},{6,5},{7,6},{0,7},{9,8},{10,9},{11,1... | collective-permute-start | bytes 73736 | tf_op jit(solution)/shard_map/ppermute | solution.py:22
  114.0 5.1 %collective-permute-start.20 = (f32[3,8,256]{2,1,0:T(8,128)S(1)}, f32[3,8,256]{2,1,0:T(8,128)S(1)}, u32[]{:S(2)}, u32[]{:S(2)}) collective-permute-start(f32[3,8,256]{2,1,0:T(8,128)S(1)} %get-tuple-element.362), channel_id=1, source_target_pairs={{0,1},{1,2},{2,3},{3,4},{4,5},{5,6},{6,7},{7,0},{8,9},{9,10},{10,1... | collective-permute-start | bytes 73736 | tf_op jit(solution)/shard_map/ppermute | solution.py:19
  127.2 1.6 %collective-permute-start.23 = (f32[3,6,256]{2,1,0:T(8,128)S(1)}, f32[3,6,256]{2,1,0:T(8,128)S(1)}, u32[]{:S(2)}, u32[]{:S(2)}) collective-permute-start(f32[3,6,256]{2,1,0:T(8,128)S(1)} %get-tuple-element.361), channel_id=1, source_target_pairs={{1,0},{2,1},{3,2},{4,3},{5,4},{6,5},{7,6},{0,7},{9,8},{10,9},{11,1... | collective-permute-start | bytes 55304 | tf_op jit(solution)/shard_map/ppermute | solution.py:22
  127.3 5.1 %collective-permute-start.22 = (f32[3,6,256]{2,1,0:T(8,128)S(1)}, f32[3,6,256]{2,1,0:T(8,128)S(1)}, u32[]{:S(2)}, u32[]{:S(2)}) collective-permute-start(f32[3,6,256]{2,1,0:T(8,128)S(1)} %get-tuple-element.360), channel_id=1, source_target_pairs={{0,1},{1,2},{2,3},{3,4},{4,5},{5,6},{6,7},{7,0},{8,9},{9,10},{10,1... | collective-permute-start | bytes 55304 | tf_op jit(solution)/shard_map/ppermute | solution.py:19
